TPU v7x, 8 devices: a whole 2x2x1 slice. The times are simulated.
8 devices in a mesh: dp: 1 (over z), ep: 2 (over y), tp: 4 (over x, core).
Axes of the slice: x: 2, y: 2, z: 1, core: 2. Of those that a mesh axis runs over, the one named last changes fastest.
Arguments:
- tokens: bfloat16 [1024, 896], P(('dp', 'ep', 'tp'))
- expert_ids: int32 [1024, 8], P(('dp', 'ep', 'tp'))
- gates: float32 [1024, 8], P(('dp', 'ep', 'tp'))
- w_gate: bfloat16 [64, 896, 2560], P('ep', None, 'tp')
- w_up: bfloat16 [64, 896, 2560], P('ep', None, 'tp')
- w_down: bfloat16 [64, 2560, 896], P('ep', 'tp')
Outputs:
- output: bfloat16 [1024, 896], P(('dp', 'ep', 'tp'))
All inputs are finite; a program needn't handle non-finite values.
Results may differ from a plain program's by a relative error of at most 0.0102111.
Values are sent between devices in bfloat16 or wider.
A program may use at most 1 GiB of HBM per device.

v0:
```python
import jax
import jax.numpy as jnp
from jax import lax
from jax.sharding import PartitionSpec as P


def slot_numbers(routes, experts):
    hit_count = jnp.sum((routes[:, :, None] == jnp.arange(experts)).astype(jnp.int32), axis=1)
    before = jnp.cumsum(hit_count, axis=0) - hit_count
    return jnp.take_along_axis(before, routes, axis=1)


def dispatch_rows(dev_rows, dest_slot, total_slots):
    row_ids = jnp.broadcast_to(jnp.arange(dev_rows.shape[0], dtype=jnp.int32)[:, None], dest_slot.shape)
    owner_row = jnp.full((total_slots,), dev_rows.shape[0], jnp.int32).at[dest_slot.reshape(-1)].set(row_ids.reshape(-1), mode="drop")
    return jnp.take(dev_rows, owner_row, axis=0, mode="fill", fill_value=0)


def combine_rows(out_table, dest_slot, kept_mask, dev_gates):
    picked = jnp.take(out_table, dest_slot, axis=0, mode="fill", fill_value=0)
    gate_kept = jnp.where(kept_mask, dev_gates, 0.0)
    return jnp.sum(gate_kept[:, :, None] * picked, axis=1).astype(jnp.bfloat16)


def solution(mesh):
    ep_size = mesh.shape["ep"]
    tp_size = mesh.shape["tp"]
    row_spec = P(("dp", "ep", "tp"), None)

    def local_layer(tokens, expert_ids, gates, w_gate, w_up, w_down):
        tok_dev, d_model = tokens.shape
        top_k = expert_ids.shape[1]
        local_experts = w_gate.shape[0]
        experts = local_experts * ep_size
        capacity = 5 * top_k * tok_dev // (4 * experts)
        slot_ids = slot_numbers(expert_ids, experts)
        kept_mask = slot_ids < capacity
        dest_slot = jnp.where(kept_mask, expert_ids * capacity + slot_ids, experts * capacity)
        send_rows = dispatch_rows(tokens, dest_slot, experts * capacity).reshape(experts, capacity, d_model)
        recv_rows = lax.all_to_all(send_rows, "ep", 0, 1, tiled=True)
        group_rows = lax.all_gather(recv_rows, "tp", axis=1, tiled=True)
        act_gate = jnp.einsum("erd,edf->erf", group_rows, w_gate, preferred_element_type=jnp.float32)
        act_up = jnp.einsum("erd,edf->erf", group_rows, w_up, preferred_element_type=jnp.float32)
        hidden = (jax.nn.silu(act_gate) * act_up).astype(jnp.bfloat16)
        partial_out = jnp.einsum("erf,efd->erd", hidden, w_down, preferred_element_type=jnp.float32).astype(jnp.bfloat16)
        partial_out = partial_out.reshape(local_experts, tp_size, ep_size * capacity, d_model)
        partial_in = lax.all_to_all(partial_out, "tp", 1, 1, tiled=True)
        out_rows = jnp.sum(partial_in.astype(jnp.float32), axis=1).astype(jnp.bfloat16)
        back_rows = lax.all_to_all(out_rows, "ep", 1, 0, tiled=True)
        return combine_rows(back_rows.reshape(experts * capacity, d_model), dest_slot, kept_mask, gates)

    return jax.shard_map(
        local_layer,
        mesh=mesh,
        in_specs=(row_spec, row_spec, row_spec, P("ep", None, "tp"), P("ep", None, "tp"), P("ep", "tp", None)),
        out_specs=row_spec,
        check_vma=False,
    )
```

profile of v0, /device:TPU:0, one launch (start us, length us, event | category | flops | bytes accessed | tf_op | source)
XLA Modules:
  0.0 363.3 jit_solution(13771719410114858445)
XLA Ops:
  6.5 0.0 copy-start
  6.5 0.0 all-gather.2.cloned.1.call-start
  6.5 0.8 convert_reduce_fusion
  7.3 0.7 bitcast_or_fusion
  8.0 0.1 copy.72
  8.1 0.2 reduce_window_sum.11
  8.3 0.1 copy.74
  8.4 0.1 reshape.90
  8.5 0.0 copy-start.2
  8.5 7.1 %gather_fusion.2 = s32[1024]{0:T(1024)S(1)} fusion(s32[128,64]{1,0:T(8,128)S(1)} %sub.3, s32[1024]{0:T(1024)S(1)} %reshape.90), kind=kCustom, calls=%fused_computation.2 | custom fusion | bytes 16384 | tf_op jit(solution)/shard_map/jit(take_along_axis)/gather | solution.py:10
  15.6 0.1 reshape.93
  15.7 0.0 copy-done.2
  15.7 0.1 copy.78
  15.8 0.1 reshape.70
  16.0 0.1 reshape.100
  16.1 4.3 %scatter_custom_fusion = s32[1280]{0:T(1024)S(1)} fusion(s32[1024]{0:T(1024)S(1)} %bitcast.31, s32[1024]{0:T(1024)S(1)} %reshape.100, s32[]{:T(128)} %constant.57.clone.1), kind=kCustom, calls=%fused_computation.20 | custom fusion | bytes 5124 | tf_op jit(solution)/shard_map/scatter | solution.py:15
  20.4 0.0 copy-done
  20.4 5.0 %gather_fusion = bf16[1280,896]{1,0:T(8,128)(2,1)} fusion(bf16[128,896]{1,0:T(8,128)(2,1)S(1)} %copy-done, s32[2048]{0:T(1024)S(1)} %pad_clamp_fusion), kind=kCustom, calls=%fused_computation | custom fusion | bytes 4592640 | tf_op jit(solution)/shard_map/jit(_take)/gather | solution.py:16
  25.4 3.4 gather.16
  28.8 0.1 broadcast_in_dim.57
  28.9 0.4 broadcast_select_fusion
  29.3 36.4 %all_to_all.38 = bf16[64,20,896]{2,1,0:T(8,128)(2,1)S(1)} all-to-all(bf16[64,20,896]{2,1,0:T(8,128)(2,1)S(1)} %broadcast_select_fusion), channel_id=1, replica_groups=mesh['dp'=1,'ep'=2,'tp'=4] {'ep'}, dimensions={0} | all-to-all | bytes 4587520 | tf_op jit(solution)/shard_map/all_to_all | solution.py:40
  65.7 0.3 copy.80
  66.0 2.1 copy.81
  68.1 0.0 all-gather.2.cloned.1.call-update
  68.1 60.7 %all-gather.2.cloned.1.call-done = bf16[32,160,896]{2,1,0:T(8,128)(2,1)} async-done(((bf16[32,40,896]{2,1,0:T(8,128)(2,1)}), bf16[32,160,896]{2,1,0:T(8,128)(2,1)}) %all-gather.2.cloned.1.call-update) | async-done | bytes 9175056 | tf_op jit(solution)/shard_map/all_gather | solution.py:41
  128.8 21.9 %fusion.7 = f32[32,160,640]{2,1,0:T(8,128)} fusion(bf16[32,160,896]{2,1,0:T(8,128)(2,1)} %all-gather.2.cloned.1.call-done, bf16[32,896,640]{2,1,0:T(8,128)(2,1)} %param.9), kind=kOutput, calls=%fused_computation.29 | convolution fusion | flops 5872025600 | bytes 58982400 | tf_op jit(solution)/shard_map/erd,edf->erf/dot_general | solution.py:42
  150.7 35.6 %fusion.1 = bf16[32,160,896]{2,1,0:T(8,128)(2,1)} fusion(bf16[32,640,896]{2,1,0:T(8,128)(2,1)} %param.11, f32[32,160,640]{2,1,0:T(8,128)} %fusion.7, bf16[32,160,896]{2,1,0:T(8,128)(2,1)} %all-gather.2.cloned.1.call-done, bf16[32,896,640]{2,1,0:T(8,128)(2,1)} %param.10), kind=kOutput, calls=%fused_computation.6 | convolution fusion | flops 11768299520 | bytes 104857600 | tf_op jit(solution)/shard_map/erf,efd->erd/dot_general | solution.py:45
  186.3 7.9 %copy.82 = bf16[32,4,40,896]{3,2,0,1:T(8,128)(2,1)} copy(bf16[32,4,40,896]{3,2,1,0:T(8,128)(2,1)} %bitcast.30) | data formatting | bytes 18350080 | tf_op jit(solution)/shard_map/reshape | solution.py:46
  194.1 109.3 %all_to_all.39 = bf16[32,4,40,896]{3,2,0,1:T(8,128)(2,1)} all-to-all(bf16[32,4,40,896]{3,2,0,1:T(8,128)(2,1)} %copy.82), channel_id=1, replica_groups=mesh['dp'=1,'ep'=2,'tp'=4] {'tp'}, dimensions={1} | all-to-all | bytes 18350080 | tf_op jit(solution)/shard_map/all_to_all | solution.py:47
  303.4 0.0 copy-start.3
  303.4 6.3 %reduce_sum.31 = bf16[32,40,896]{2,1,0:T(8,128)(2,1)S(1)} reduce(bf16[32,4,40,896]{3,2,0,1:T(8,128)(2,1)} %all_to_all.39, bf16[]{:T(256)} %constant.59.clone.1), dimensions={1}, to_apply=%region_3.4 | reduce | flops 3440640 | bytes 11468802 | tf_op jit(solution)/shard_map/reduce_sum | solution.py:48
  309.7 1.7 copy.84
  311.4 3.8 %all-to-all-start.2 = ((bf16[32,40,896]{2,0,1:T(8,128)(2,1)}), bf16[32,40,896]{2,0,1:T(8,128)(2,1)S(1)}, u32[]{:S(2)}, u32[]{:S(2)}) async-start(bf16[32,40,896]{2,0,1:T(8,128)(2,1)} %copy.84), calls=%async_computation.2 | async-start | bytes 4587520 | tf_op jit(solution)/shard_map/all_to_all | solution.py:49
  315.2 0.1 copy.86
  315.3 0.1 reshape.84
  315.4 0.1 copy.77
  315.5 0.0 copy-done.3
  315.5 0.1 copy.76
  315.6 26.2 %all-to-all-done.2 = bf16[32,40,896]{2,0,1:T(8,128)(2,1)S(1)} async-done(((bf16[32,40,896]{2,0,1:T(8,128)(2,1)}), bf16[32,40,896]{2,0,1:T(8,128)(2,1)S(1)}, u32[]{:S(2)}, u32[]{:S(2)}) %all-to-all-start.2) | async-done | bytes 2293792 | tf_op jit(solution)/shard_map/all_to_all | solution.py:49
  341.8 2.4 copy.85
  344.2 0.0 copy-start.1
  344.2 3.5 reshape.73
  347.7 5.3 %gather_fusion.1 = bf16[1024,896]{1,0:T(8,128)(2,1)} fusion(bf16[1280,896]{1,0:T(8,128)(2,1)S(1)} %reshape.73, s32[1024]{0:T(1024)S(1)} %broadcast_clamp_fusion), kind=kCustom, calls=%fused_computation.1 | custom fusion | bytes 3674112 | tf_op jit(solution)/shard_map/jit(_take)/gather | solution.py:20
  352.9 3.5 multiply_reduce_fusion
  356.5 0.0 copy-done.1
  (11 shorter events, 0.1 us)
Async XLA Ops:
  6.5 13.9 %copy-start = (bf16[128,896]{1,0:T(8,128)(2,1)S(1)}, bf16[128,896]{1,0:T(8,128)(2,1)}, u32[]{:S(2)}) copy-start(bf16[128,896]{1,0:T(8,128)(2,1)} %param.6) | copy-start | bytes 688132
  6.5 122.2 %all-gather.2.cloned.1.call-start = ((), (), s32[]{:S(2)}) async-start(), calls=%async_computation.3 | async-start | bytes 11468800 | tf_op jit(solution)/shard_map/all_gather | solution.py:41
  8.5 7.2 %copy-start.2 = (s32[128,8]{0,1:T(8,128)S(1)}, s32[128,8]{0,1:T(8,128)}, u32[]{:S(2)}) copy-start(s32[128,8]{0,1:T(8,128)} %param.7) | copy-start | bytes 12292
  303.4 12.1 %copy-start.3 = (f32[128,8]{0,1:T(8,128)S(1)}, f32[128,8]{0,1:T(8,128)}, u32[]{:S(2)}) copy-start(f32[128,8]{0,1:T(8,128)} %param.8) | copy-start | bytes 12292
  311.4 30.4 %all-to-all-start.2 = ((bf16[32,40,896]{2,0,1:T(8,128)(2,1)}), bf16[32,40,896]{2,0,1:T(8,128)(2,1)S(1)}, u32[]{:S(2)}, u32[]{:S(2)}) async-start(bf16[32,40,896]{2,0,1:T(8,128)(2,1)} %copy.84), calls=%async_computation.2 | async-start | bytes 4587520 | tf_op jit(solution)/shard_map/all_to_all | solution.py:49
  344.2 12.3 %copy-start.1 = (bf16[128,896]{1,0:T(8,128)(2,1)S(1)}, bf16[128,896]{1,0:T(8,128)(2,1)}, u32[]{:S(2)}) copy-start(bf16[128,896]{1,0:T(8,128)(2,1)} %param.6) | copy-start | bytes 688132
Sparse Core Ops, SparseCore 0:
  68.2 60.4 all-gather.1
where the time goes:
time: 364 us; the launch traced here: 363 us
  blocking collectives  146 us (40%)
  waiting for transfers between devices  86.8 us (24%)
  matrix products  57.5 us (16%)
  local copies, waits for them, and re-layouts  44 us (12%)
  between operations  13.6 us (4%)
  other arithmetic  11.9 us (3%)
  starting transfers between devices  3.8 us (1%)
    all_to_all x1, blocking collectives, local_layer(): partial_in = lax.all_to_all(partial_out, 'tp', 1, 1, tiled=True)  109 us
    all_gather x1, waiting for transfers between devices, local_layer(): group_rows = lax.all_gather(recv_rows, 'tp', axis=1, tiled=True)  60.7 us
    all_to_all x1, blocking collectives, local_layer(): recv_rows = lax.all_to_all(send_rows, 'ep', 0, 1, tiled=True)  36.4 us
    dot_general x1, matrix products, local_layer(): jnp.einsum('erf,efd->erd', hidden, w_down, preferred_element_type=jnp.flo...  35.6 us
    all_to_all x1, waiting for transfers between devices, local_layer(): back_rows = lax.all_to_all(out_rows, 'ep', 1, 0, tiled=True)  26.2 us
    dot_general x1, matrix products, local_layer(): jnp.einsum('erd,edf->erf', group_rows, w_gate, preferred_element_type=jnp...  21.9 us
    gather x2, local copies, waits for them, and re-layouts, dispatch_rows(): return jnp.take(dev_rows, owner_row, axis=0, mode='fill', fill_value=0)  8.33 us
    reshape x1, local copies, waits for them, and re-layouts, local_layer(): partial_out.reshape(local_experts, tp_size, ep_size * capacity, d_model)  7.85 us
  transfers between devices with their start and end apart: 2, of which 2 were waited for; matrix products, arithmetic and copies ran while one was open for 0% of the time, Pallas kernels for 0%

commit v1 on v0

v1 whole, which is shorter than its diff:
```python
import functools

import jax
import jax.numpy as jnp
from jax import lax
from jax.experimental import pallas as pl
from jax.experimental.pallas import tpu as pltpu
from jax.sharding import PartitionSpec as P

MESH = pl.DeviceIdType.MESH
BF16 = jnp.bfloat16
F32 = jnp.float32

SOURCES = 8
MAIN = 16
BLOCK = 4
RING = 12
WIDE = 256
NO_SLOT = 255.0

TO_PARTNER, X_LOW, X_HIGH, Y_HIGH, Y_LOW, DIAG_Y, DIAG_X, PASS_X, PASS_Y, PASS_D = range(10)
META_P, META_X, META_Y, META_D, META_PX, META_PY, META_PD = range(10, 17)
FIRST_SUM = 17
OWN, XN, DIAG, YN = range(4)
PLACE = (OWN, XN, YN, DIAG)


def iota(shape, dim):
    return lax.broadcasted_iota(jnp.int32, shape, dim)


def kernel(
    ids_ref, gates_ref, tok_hbm, wg_hbm, wu_hbm, wd_hbm, out_ref,
    xg, mg, val, spread, gmat, xe, hid, ring, away, home, got, rx1, ry1, rx2, ry2, via_x, via_y,
    own_sem, wsem, ssem, rsem,
):
    top_k, tok = ids_ref.shape
    experts = wg_hbm.shape[0]
    d_model, ff = wg_hbm.shape[1:]
    half = tok // 2
    rest = 4
    ep, tp = lax.axis_index("ep"), lax.axis_index("tp")
    partner = {"tp": tp + 1 - 2 * (tp % 2)}
    xn = {"tp": (tp + 2) % 4}
    yn = {"ep": 1 - ep}
    first_expert = ep * experts

    chunks = []
    start = 0
    while start < d_model:
        chunks.append((start, min(WIDE, d_model - start)))
        start += WIDE
    n_chunks = len(chunks)

    per_slot = 4
    groups = experts // per_slot

    def load_up(e, slot):
        return [
            pltpu.make_async_copy(wg_hbm.at[e], ring.at[slot, 0], wsem.at[slot, 0]),
            pltpu.make_async_copy(wu_hbm.at[e], ring.at[slot, 1], wsem.at[slot, 1]),
        ]

    def down_view(slot, k, width):
        per_plane = 2 if width == WIDE else 4
        return ring.at[slot, k // per_plane, pl.ds(0, ff), pl.ds((k % per_plane) * width, width)]

    def load_down(first, column, width, slot):
        count = per_slot if width == WIDE else 2 * per_slot
        return [
            pltpu.make_async_copy(
                wd_hbm.at[first + k, :, pl.ds(column, width)], down_view(slot, k, width), wsem.at[slot, k]
            )
            for k in range(count)
        ]

    n_up = experts // BLOCK
    per_chunk = groups // BLOCK

    def down_block(b):
        lb = b - n_up
        c = lb // per_chunk if lb < per_chunk * (n_chunks - 1) else n_chunks - 1
        return c, (lb - c * per_chunk) * BLOCK * per_slot

    def start_down(b):
        c, first = down_block(b)
        column, width = chunks[c]
        step = per_slot if width == WIDE else 2 * per_slot
        for i in range(BLOCK):
            for copy in load_down(first + i * step, column, width, (b * BLOCK + i) % RING):
                copy.start()

    for s in range(RING):
        for copy in load_up(s, s):
            copy.start()
    own = pltpu.make_async_copy(tok_hbm, xg.at[0], own_sem)
    own.start()

    mg[0, 0:top_k, :] = ids_ref[...].astype(F32)
    mg[0, top_k:, :] = gates_ref[...]

    def message(i, src, dst, dev):
        return pltpu.make_async_remote_copy(
            src_ref=src, dst_ref=dst, send_sem=ssem.at[i], recv_sem=rsem.at[i], device_id=dev, device_id_type=MESH
        )

    low, high = pl.ds(0, half), pl.ds(half, half)
    sent = {
        TO_PARTNER: message(TO_PARTNER, xg.at[0], xg.at[1], partner),
        X_LOW: message(X_LOW, xg.at[0, low], xg.at[2, low], xn),
        X_HIGH: message(X_HIGH, xg.at[0, high], xg.at[2, high], xn),
        Y_HIGH: message(Y_HIGH, xg.at[0, high], xg.at[4, high], yn),
        Y_LOW: message(Y_LOW, xg.at[0, low], xg.at[4, low], yn),
        DIAG_Y: message(DIAG_Y, xg.at[2, low], xg.at[6, low], yn),
        DIAG_X: message(DIAG_X, xg.at[4, high], xg.at[6, high], xn),
        PASS_X: message(PASS_X, xg.at[2], xg.at[3], partner),
        PASS_Y: message(PASS_Y, xg.at[4], xg.at[5], partner),
        PASS_D: message(PASS_D, xg.at[6], xg.at[7], partner),
        META_P: message(META_P, mg.at[0], mg.at[1], partner),
        META_X: message(META_X, mg.at[0], mg.at[2], xn),
        META_Y: message(META_Y, mg.at[0], mg.at[4], yn),
        META_D: message(META_D, mg.at[2], mg.at[6], yn),
        META_PX: message(META_PX, mg.at[2], mg.at[3], partner),
        META_PY: message(META_PY, mg.at[4], mg.at[5], partner),
        META_PD: message(META_PD, mg.at[6], mg.at[7], partner),
    }

    barrier = pltpu.get_barrier_semaphore()
    for dev in (partner, xn, yn):
        pl.semaphore_signal(barrier, inc=1, device_id=dev, device_id_type=MESH)
    row, col = iota(spread.shape, 0), iota(spread.shape, 1)
    spread[...] = jnp.where(row == col // MAIN, 1.0, 0.0).astype(BF16)
    pl.semaphore_wait(barrier, 3)
    for i in (META_P, META_X, META_Y):
        sent[i].start()
    own.wait()
    for i in (X_LOW, Y_HIGH, X_HIGH, Y_LOW, TO_PARTNER):
        sent[i].start()

    earlier = jnp.where(iota((tok, tok), 0) < iota((tok, tok), 1), 1.0, 0.0).astype(BF16)
    expert_row = (iota((experts, tok), 0) + first_expert).astype(F32)
    n_main = experts * MAIN
    lane = iota((tok, n_main), 1)

    def route(r):
        hit = jnp.zeros((experts, tok), F32)
        gate = jnp.zeros((experts, tok), F32)
        for j in range(top_k):
            here = mg[r, j : j + 1, :] == expert_row
            hit = jnp.where(here, 1.0, hit)
            gate = jnp.where(here, mg[r, top_k + j : top_k + j + 1, :], gate)
        before = jnp.dot(hit.astype(BF16), earlier, preferred_element_type=F32)
        slot = jnp.where(hit > 0.5, before, NO_SLOT)
        val[r] = slot
        g_hi = gate.astype(BF16).astype(F32)
        g_mid = (gate - g_hi).astype(BF16).astype(F32)
        g_lo = gate - g_hi - g_mid
        stack = jnp.concatenate([slot, g_hi, g_mid, g_lo], axis=0)
        by_token = stack.T.astype(BF16)
        wide = jnp.dot(by_token, spread[...], preferred_element_type=F32)
        slot_of = wide[:, 0:n_main]
        in_main = slot_of == (lane % MAIN).astype(F32)
        mine = (lane % MAIN) // rest == r % 4
        in_rest = slot_of == jnp.where(mine, MAIN + lane % rest, -1).astype(F32)
        for k in range(3):
            piece = wide[:, (k + 1) * n_main : (k + 2) * n_main]
            rows = pl.ds(k * tok, tok)
            gmat[r, rows, 0:n_main] = jnp.where(in_main, piece, 0.0).astype(BF16)
            gmat[r, rows, n_main:] = jnp.where(in_rest, piece, 0.0).astype(BF16)

    def one_hot(slots, want, e):
        line = jnp.broadcast_to(slots[e : e + 1, :], want.shape)
        return jnp.where(line == want, 1.0, 0.0).astype(BF16)

    def dispatch(sources, want, rows, batch):
        slots = jnp.concatenate([val[r] for r in sources], axis=1)
        x = xg[sources[0] : sources[-1] + 1].reshape(len(sources) * tok, d_model)
        height = want.shape[0]
        for e in range(0, experts, batch):
            pick = jnp.concatenate([one_hot(slots, want, e + i) for i in range(batch)], axis=0)
            placed = jnp.dot(pick, x, preferred_element_type=F32).astype(BF16)
            xe[e : e + batch, rows : rows + height, :] = placed.reshape(batch, height, d_model)

    def dispatch_pair(p):
        shape = (2 * MAIN, 2 * tok)
        i, l = iota(shape, 0), iota(shape, 1)
        want = jnp.where(i // MAIN == l // tok, i % MAIN, -1).astype(F32)
        dispatch([2 * p, 2 * p + 1], want, 2 * MAIN * p, 8)

    def dispatch_rest(q):
        shape = (4 * rest, 4 * tok)
        i, l = iota(shape, 0), iota(shape, 1)
        want = jnp.where(i // rest == l // tok, MAIN + i % rest, -1).astype(F32)
        dispatch([4 * q + i for i in range(4)], want, MAIN * SOURCES + 4 * rest * q, 16)

    def route_range(lo, hi):
        @pl.loop(lo, hi)
        def _(r):
            route(r)

    sent[META_P].wait_recv()
    route_range(0, 2)
    sent[TO_PARTNER].wait_recv()
    dispatch_pair(0)
    sent[META_X].wait_recv()
    sent[META_D].start()
    sent[META_PX].start()
    sent[META_Y].wait_recv()
    sent[META_PY].start()
    sent[X_LOW].wait_recv()
    sent[DIAG_Y].start()
    sent[Y_HIGH].wait_recv()
    sent[DIAG_X].start()
    sent[META_D].wait_recv()
    sent[META_PD].start()
    sent[META_PX].wait_recv()
    sent[META_PY].wait_recv()
    route_range(2, 6)
    sent[X_HIGH].wait_recv()
    sent[PASS_X].start()
    sent[Y_LOW].wait_recv()
    sent[PASS_Y].start()
    sent[META_PD].wait_recv()
    route_range(6, 8)
    sent[PASS_X].wait_recv()
    dispatch_pair(1)
    sent[PASS_Y].wait_recv()
    dispatch_pair(2)
    sent[DIAG_Y].wait_recv()
    sent[DIAG_X].wait_recv()
    sent[PASS_D].start()
    dispatch_rest(0)
    sent[PASS_D].wait_recv()
    dispatch_pair(3)
    dispatch_rest(1)

    full = ff // WIDE * WIDE

    def up_block(b):
        base = (b * BLOCK) % RING
        for i in range(BLOCK):
            for copy in load_up(b * BLOCK + i, base + i):
                copy.wait()
        for i in range(BLOCK):
            e, slot = b * BLOCK + i, base + i
            x = xe[e]
            a = jnp.dot(x, ring[slot, 0, :, 0:full], preferred_element_type=F32)
            u = jnp.dot(x, ring[slot, 1, :, 0:full], preferred_element_type=F32)
            hid[e, :, 0:full] = (jax.nn.silu(a) * u).astype(BF16)
            tail = jnp.concatenate([ring[slot, 0, :, full:], ring[slot, 1, :, full:]], axis=1)
            t = jnp.dot(x, tail, preferred_element_type=F32)
            hid[e, :, full:] = (jax.nn.silu(t[:, : ff - full]) * t[:, ff - full :]).astype(BF16)

    ahead = RING // BLOCK

    @pl.loop(0, n_up - ahead)
    def _(b):
        up_block(b)
        for i in range(BLOCK):
            for copy in load_up((b + ahead) * BLOCK + i, (b * BLOCK) % RING + i):
                copy.start()

    for b in range(n_up - ahead, n_up):
        up_block(b)
        start_down(b + ahead)

    n_blocks = n_up + per_chunk * (n_chunks - 1) + 1

    def down(b, lo, hi):
        c, first = down_block(b)
        column, width = chunks[c]
        step = per_slot if width == WIDE else 2 * per_slot
        put = (c % 2) * WIDE
        for i in range(lo, hi):
            for copy in load_down(first + i * step, column, width, (b * BLOCK + i) % RING):
                copy.wait()
        for i in range(lo, hi):
            for k in range(step):
                e = first + i * step + k
                w = down_view((b * BLOCK + i) % RING, k, width)[...]
                y = jnp.dot(hid[e], w, preferred_element_type=F32)
                xe[e, :, put : put + width] = y.astype(BF16)
        if hi == BLOCK and b + ahead < n_blocks:
            start_down(b + ahead)

    def gated(r, c):
        width = chunks[c][1]
        put = (c % 2) * WIDE
        top = MAIN * r
        bottom = MAIN * SOURCES + 4 * rest * (r // 4)
        y = jnp.concatenate(
            [
                xe[:, top : top + MAIN, put : put + width].reshape(n_main, width),
                xe[:, bottom : bottom + 4 * rest, put : put + width].reshape(n_main, width),
            ],
            axis=0,
        )
        s = jnp.dot(gmat[r], y, preferred_element_type=F32)
        return s[0:tok] + s[tok : 2 * tok] + s[2 * tok :]

    def cols(c):
        return pl.ds(*chunks[c])

    def sums(kind, c):
        i = FIRST_SUM + 5 * c + kind
        if kind == 0:
            return message(i, away.at[:, :, cols(c)], got.at[:, :, cols(c)], partner)
        if kind == 1:
            return message(i, home.at[pl.ds(XN, 2), low, cols(c)], rx1.at[:, :, cols(c)], xn)
        if kind == 2:
            return message(i, home.at[pl.ds(DIAG, 2), high, cols(c)], ry1.at[:, :, cols(c)], yn)
        if kind == 3:
            return message(i, via_y.at[:, cols(c)], ry2.at[:, cols(c)], yn)
        return message(i, via_x.at[:, cols(c)], rx2.at[:, cols(c)], xn)

    def combine_away(c):
        for r in range(1, SOURCES, 2):
            away[PLACE[r // 2], :, cols(c)] = gated(r, c)

    def combine_home(c):
        sums(0, c).start()
        for r in range(0, SOURCES, 2):
            home[PLACE[r // 2], :, cols(c)] = gated(r, c)

    def chip_sum(c):
        sums(0, c).wait_recv()
        for d in range(4):
            home[d, :, cols(c)] += got[d, :, cols(c)]
        sums(1, c).start()
        sums(2, c).start()

    def pass_on(c):
        sums(1, c).wait_recv()
        via_y[:, cols(c)] = home[YN, low, cols(c)] + rx1[1, :, cols(c)]
        sums(3, c).start()
        sums(2, c).wait_recv()
        via_x[:, cols(c)] = home[XN, high, cols(c)] + ry1[0, :, cols(c)]
        sums(4, c).start()

    def finish(c):
        sums(3, c).wait_recv()
        out_ref[low, cols(c)] = (home[OWN, low, cols(c)] + rx1[0, :, cols(c)] + ry2[:, cols(c)]).astype(BF16)
        sums(4, c).wait_recv()
        out_ref[high, cols(c)] = (home[OWN, high, cols(c)] + ry1[1, :, cols(c)] + rx2[:, cols(c)]).astype(BF16)

    b = n_up
    for c in range(n_chunks):
        if c < n_chunks - 1:
            parts = [(b + i, 0, BLOCK) for i in range(per_chunk)]
            b += per_chunk
        else:
            parts = [(b, 0, BLOCK // 2), (b, BLOCK // 2, BLOCK)]
        for n, part in enumerate(parts):
            down(*part)
            if n == 0 and c >= 1:
                chip_sum(c - 1)
            if n == 1 and c >= 2:
                pass_on(c - 2)
        combine_away(c)
        combine_home(c)
    last = n_chunks - 1
    chip_sum(last)
    pass_on(last - 1)
    for c in range(last - 1):
        finish(c)
    pass_on(last)
    finish(last - 1)
    finish(last)

    for i in range(FIRST_SUM):
        sent[i].wait_send()
    for c in range(n_chunks):
        for kind in range(5):
            sums(kind, c).wait_send()


def solution(mesh):
    ep_size, tp_size = mesh.shape["ep"], mesh.shape["tp"]
    row_spec = P(("dp", "ep", "tp"), None)

    def local_layer(tokens, expert_ids, gates, w_gate, w_up, w_down):
        tok, d_model = tokens.shape
        top_k = expert_ids.shape[1]
        experts, _, ff = w_gate.shape
        capacity = 5 * top_k * tok // (4 * experts * ep_size)
        assert (ep_size, tp_size, capacity, tok, experts) == (2, 4, MAIN + 4, 128, 32)
        n_main = experts * MAIN
        rows = SOURCES * capacity
        n_chunks = -(-d_model // WIDE)
        n_msg = FIRST_SUM + 5 * n_chunks
        vmem = pl.BlockSpec(memory_space=pltpu.VMEM)
        hbm = pl.BlockSpec(memory_space=pl.ANY)
        return pl.pallas_call(
            kernel,
            out_shape=jax.ShapeDtypeStruct((tok, d_model), BF16),
            in_specs=[vmem, vmem, hbm, hbm, hbm, hbm],
            out_specs=vmem,
            scratch_shapes=[
                pltpu.VMEM((SOURCES, tok, d_model), BF16),
                pltpu.VMEM((SOURCES, 2 * top_k, tok), F32),
                pltpu.VMEM((SOURCES, experts, tok), F32),
                pltpu.VMEM((4 * experts, 4 * n_main), BF16),
                pltpu.VMEM((SOURCES, 3 * tok, 2 * n_main), BF16),
                pltpu.VMEM((experts, rows, d_model), BF16),
                pltpu.VMEM((experts, rows, ff), BF16),
                pltpu.VMEM((RING, 2, d_model, ff), BF16),
                pltpu.VMEM((4, tok, d_model), F32),
                pltpu.VMEM((4, tok, d_model), F32),
                pltpu.VMEM((4, tok, d_model), F32),
                pltpu.VMEM((2, tok // 2, d_model), F32),
                pltpu.VMEM((2, tok // 2, d_model), F32),
                pltpu.VMEM((tok // 2, d_model), F32),
                pltpu.VMEM((tok // 2, d_model), F32),
                pltpu.VMEM((tok // 2, d_model), F32),
                pltpu.VMEM((tok // 2, d_model), F32),
                pltpu.SemaphoreType.DMA,
                pltpu.SemaphoreType.DMA((RING, 8)),
                pltpu.SemaphoreType.DMA((n_msg,)),
                pltpu.SemaphoreType.DMA((n_msg,)),
            ],
            compiler_params=pltpu.CompilerParams(
                collective_id=0, has_side_effects=True, vmem_limit_bytes=67043328
            ),
        )(expert_ids.T, gates.T, tokens, w_gate, w_up, w_down)

    return jax.shard_map(
        local_layer,
        mesh=mesh,
        in_specs=(row_spec, row_spec, row_spec, P("ep", None, "tp"), P("ep", None, "tp"), P("ep", "tp", None)),
        out_specs=row_spec,
        check_vma=False,
    )
```

time: 364 us -> 73.8 us (0.20)
  blocking collectives: 146 us -> 0 us
  waiting for transfers between devices: 86.8 us -> 0 us
  Pallas kernels: 0 us -> 71.9 us
  matrix products: 57.5 us -> 0 us
  local copies, waits for them, and re-layouts: 44 us -> 1.65 us
  between operations: 13.6 us -> 0.01 us
  other arithmetic: 11.9 us -> 0 us
  starting transfers between devices: 3.8 us -> 0 us
    all_to_all x2 -> x0, blocking collectives: 146 us -> none  [the longest x1 109 us: local_layer(): partial_in = lax.all_to_all(partial_out, 'tp', 1, 1, tiled=True)]
    pallas_call x0 -> x1, Pallas kernels: none -> 71.9 us  [local_layer(): pl.pallas_call(kernel, out_shape=jax.ShapeDtypeStruct((tok, d_model), BF1...]
    all_gather x1 -> x0, waiting for transfers between devices: 60.7 us -> none  [local_layer(): group_rows = lax.all_gather(recv_rows, 'tp', axis=1, tiled=True)]
    dot_general x2 -> x0, matrix products: 57.5 us -> none  [the longest x1 35.6 us: local_layer(): jnp.einsum('erf,efd->erd', hidden, w_down, preferred_element_type=jnp.flo...]
    all_to_all x1 -> x0, waiting for transfers between devices: 26.2 us -> none  [local_layer(): back_rows = lax.all_to_all(out_rows, 'ep', 1, 0, tiled=True)]
    gather x8 -> x0, local copies, waits for them, and re-layouts: 21 us -> none  [the longest x2 8.33 us: dispatch_rows(): return jnp.take(dev_rows, owner_row, axis=0, mode='fill', fill_value=0)]
    reshape x4 -> x0, local copies, waits for them, and re-layouts: 11.5 us -> none  [the longest x1 7.85 us: local_layer(): partial_out.reshape(local_experts, tp_size, ep_size * capacity, d_model)]
    reduce_sum x3 -> x0, other arithmetic: 10.6 us -> none  [the longest x1 6.27 us: local_layer(): jnp.sum(partial_in.astype(jnp.float32), axis=1).astype(jnp.bfloat16)]
  transfers between devices with their start and end apart: 2 -> 0, of which waited for: 2 -> 0; matrix products, arithmetic and copies ran while one was open for 0% -> 0% of each run, Pallas kernels for 0% -> 0%
where the time goes in v1:
time: 73.8 us; the launch traced here: 73.6 us
  Pallas kernels  71.9 us (97%)
  local copies, waits for them, and re-layouts  1.65 us (2%)
    pallas_call x1, Pallas kernels, local_layer(): pl.pallas_call(kernel, out_shape=jax.ShapeDtypeStruct((tok, d_model), BF1...  71.9 us
    unnamed x1, local copies, waits for them, and re-layouts  1.65 us

profile of v1, /device:TPU:0, one launch (start us, length us, event | category | flops | bytes accessed | tf_op | source)
XLA Modules:
  0.0 73.6 jit_solution(5122310358969478754)
XLA Ops:
  0.0 71.9 %shard_map.64 = bf16[128,896]{1,0:T(8,128)(2,1)} custom-call(s32[8,128]{1,0:T(8,128)} %bitcast.2, f32[8,128]{1,0:T(8,128)} %bitcast.3, bf16[128,896]{1,0:T(8,128)(2,1)} %tok_hbm.1, bf16[32,896,640]{2,1,0:T(8,128)(2,1)} %wg_hbm.1, bf16[32,896,640]{2,1,0:T(8,128)(2,1)} %wu_hbm.1, bf16[32,640,896]{2,1,0:T(8,128)(2,1)} %wd_hbm.1), custom_call_target="tpu_custom_call" | custom-call | tf_op jit(solution)/shard_map/pallas_call | solution.py:393
  72.0 1.6 %copy.8 = bf16[128,896]{1,0:T(8,128)(2,1)} copy(bf16[128,896]{1,0:T(8,128)(2,1)} %shard_map.64) | data formatting | bytes 458752

commit v2 on v1

--- a/solution.py
+++ b/solution.py
@@ -14,13 +14,13 @@
 SOURCES = 8
 MAIN = 16
 BLOCK = 4
-RING = 12
+RING = 16
 WIDE = 256
 NO_SLOT = 255.0
 
-TO_PARTNER, X_LOW, X_HIGH, Y_HIGH, Y_LOW, DIAG_Y, DIAG_X, PASS_X, PASS_Y, PASS_D = range(10)
-META_P, META_X, META_Y, META_D, META_PX, META_PY, META_PD = range(10, 17)
-FIRST_SUM = 17
+META = range(8)
+TO_PARTNER, X_LOW, X_HIGH, Y_HIGH, Y_LOW, DIAG_Y, DIAG_X, PASS_X, PASS_Y, PASS_D = range(8, 18)
+FIRST_SUM = 18
 OWN, XN, DIAG, YN = range(4)
 PLACE = (OWN, XN, YN, DIAG)
 
@@ -30,19 +30,20 @@
 
 
 def kernel(
-    ids_ref, gates_ref, tok_hbm, wg_hbm, wu_hbm, wd_hbm, out_ref,
-    xg, mg, val, spread, gmat, xe, hid, ring, away, home, got, rx1, ry1, rx2, ry2, via_x, via_y,
-    own_sem, wsem, ssem, rsem,
+    ids_hbm, gates_hbm, tok_hbm, wg_hbm, wu_hbm, wd_hbm, out_hbm,
+    ids_ref, gates_ref, xg, mg, val, spread, gmat, xe, yrest, ring, away, home, got, rx1, ry1, rx2, ry2, via_x, via_y, direct, result,
+    own_sem, out_sem, wsem, ssem, rsem,
 ):
-    top_k, tok = ids_ref.shape
+    top_k, tok = ids_hbm.shape
     experts = wg_hbm.shape[0]
     d_model, ff = wg_hbm.shape[1:]
     half = tok // 2
     rest = 4
     ep, tp = lax.axis_index("ep"), lax.axis_index("tp")
-    partner = {"tp": tp + 1 - 2 * (tp % 2)}
-    xn = {"tp": (tp + 2) % 4}
-    yn = {"ep": 1 - ep}
+    other = tp + 1 - 2 * (tp % 2)
+    tps = (tp, other, (tp + 2) % 4, (other + 2) % 4)
+    device = [{"ep": ep if r < 4 else 1 - ep, "tp": tps[r % 4]} for r in range(SOURCES)]
+    partner, xn, yn, diag = device[1], device[2], device[4], device[6]
     first_expert = ep * experts
 
     chunks = []
@@ -57,9 +58,16 @@
 
     def load_up(e, slot):
         return [
-            pltpu.make_async_copy(wg_hbm.at[e], ring.at[slot, 0], wsem.at[slot, 0]),
-            pltpu.make_async_copy(wu_hbm.at[e], ring.at[slot, 1], wsem.at[slot, 1]),
+            pltpu.make_async_copy(wg_hbm.at[e], ring.at[slot, 0], wsem.at[slot]),
+            pltpu.make_async_copy(wu_hbm.at[e], ring.at[slot, 1], wsem.at[slot]),
         ]
+
+    def wait_up(slot):
+        pltpu.make_async_copy(wg_hbm.at[pl.ds(0, 2)], ring.at[slot], wsem.at[slot]).wait()
+
+    def wait_down(slot):
+        area = pl.ds(0, ff), pl.ds(0, 2 * WIDE)
+        pltpu.make_async_copy(wd_hbm.at[pl.ds(0, 2), *area], ring.at[slot, :, *area], wsem.at[slot]).wait()
 
     def down_view(slot, k, width):
         per_plane = 2 if width == WIDE else 4
@@ -69,7 +77,7 @@
         count = per_slot if width == WIDE else 2 * per_slot
         return [
             pltpu.make_async_copy(
-                wd_hbm.at[first + k, :, pl.ds(column, width)], down_view(slot, k, width), wsem.at[slot, k]
+                wd_hbm.at[first + k, :, pl.ds(column, width)], down_view(slot, k, width), wsem.at[slot]
             )
             for k in range(count)
         ]
@@ -90,14 +98,16 @@
             for copy in load_down(first + i * step, column, width, (b * BLOCK + i) % RING):
                 copy.start()
 
-    for s in range(RING):
-        for copy in load_up(s, s):
-            copy.start()
-    own = pltpu.make_async_copy(tok_hbm, xg.at[0], own_sem)
-    own.start()
-
-    mg[0, 0:top_k, :] = ids_ref[...].astype(F32)
-    mg[0, top_k:, :] = gates_ref[...]
+    barrier = pltpu.get_barrier_semaphore()
+    for dev in device[1:]:
+        pl.semaphore_signal(barrier, inc=1, device_id=dev, device_id_type=MESH)
+    mine = [
+        pltpu.make_async_copy(ids_hbm, ids_ref, own_sem.at[0]),
+        pltpu.make_async_copy(gates_hbm, gates_ref, own_sem.at[1]),
+        pltpu.make_async_copy(tok_hbm, xg.at[0], own_sem.at[2]),
+    ]
+    for copy in mine:
+        copy.start()
 
     def message(i, src, dst, dev):
         return pltpu.make_async_remote_copy(
@@ -116,31 +126,33 @@
         PASS_X: message(PASS_X, xg.at[2], xg.at[3], partner),
         PASS_Y: message(PASS_Y, xg.at[4], xg.at[5], partner),
         PASS_D: message(PASS_D, xg.at[6], xg.at[7], partner),
-        META_P: message(META_P, mg.at[0], mg.at[1], partner),
-        META_X: message(META_X, mg.at[0], mg.at[2], xn),
-        META_Y: message(META_Y, mg.at[0], mg.at[4], yn),
-        META_D: message(META_D, mg.at[2], mg.at[6], yn),
-        META_PX: message(META_PX, mg.at[2], mg.at[3], partner),
-        META_PY: message(META_PY, mg.at[4], mg.at[5], partner),
-        META_PD: message(META_PD, mg.at[6], mg.at[7], partner),
     }
 
-    barrier = pltpu.get_barrier_semaphore()
-    for dev in (partner, xn, yn):
-        pl.semaphore_signal(barrier, inc=1, device_id=dev, device_id_type=MESH)
-    row, col = iota(spread.shape, 0), iota(spread.shape, 1)
-    spread[...] = jnp.where(row == col // MAIN, 1.0, 0.0).astype(BF16)
-    pl.semaphore_wait(barrier, 3)
-    for i in (META_P, META_X, META_Y):
-        sent[i].start()
-    own.wait()
+    for r in range(1, SOURCES):
+        hop = r == 1 or r % 2 == 0
+        sent[META[r]] = message(META[r], mg.at[0 if hop else r - 1], mg.at[r], device[r] if hop else partner)
+
+    for copy in mine:
+        copy.wait()
+    mg[0, 0:top_k, :] = ids_ref[...].astype(F32)
+    mg[0, top_k:, :] = gates_ref[...]
+    for s in range(RING):
+        for copy in load_up(s, s):
+            copy.start()
+    pl.semaphore_wait(barrier, SOURCES - 1)
+    for r in (6, 2, 4, 1):
+        sent[META[r]].start()
     for i in (X_LOW, Y_HIGH, X_HIGH, Y_LOW, TO_PARTNER):
         sent[i].start()
 
     earlier = jnp.where(iota((tok, tok), 0) < iota((tok, tok), 1), 1.0, 0.0).astype(BF16)
     expert_row = (iota((experts, tok), 0) + first_expert).astype(F32)
     n_main = experts * MAIN
-    lane = iota((tok, n_main), 1)
+    n_rest = experts * 2 * rest
+    row, col = iota((4 * experts, 4 * n_main), 0), iota((4 * experts, 4 * n_main), 1)
+    spread[:, 0 : 4 * n_main] = jnp.where(row == col // MAIN, 1.0, 0.0).astype(BF16)
+    row, col = iota((4 * experts, 4 * n_rest), 0), iota((4 * experts, 4 * n_rest), 1)
+    spread[:, 4 * n_main :] = jnp.where(row == col // (2 * rest), 1.0, 0.0).astype(BF16)
 
     def route(r):
         hit = jnp.zeros((experts, tok), F32)
@@ -158,14 +170,16 @@
         stack = jnp.concatenate([slot, g_hi, g_mid, g_lo], axis=0)
         by_token = stack.T.astype(BF16)
         wide = jnp.dot(by_token, spread[...], preferred_element_type=F32)
-        slot_of = wide[:, 0:n_main]
-        in_main = slot_of == (lane % MAIN).astype(F32)
-        mine = (lane % MAIN) // rest == r % 4
-        in_rest = slot_of == jnp.where(mine, MAIN + lane % rest, -1).astype(F32)
-        for k in range(3):
-            piece = wide[:, (k + 1) * n_main : (k + 2) * n_main]
-            rows = pl.ds(k * tok, tok)
+        lane = iota((tok, n_main), 1)
+        in_main = wide[:, 0:n_main] == (lane % MAIN).astype(F32)
+        lane = iota((tok, n_rest), 1)
+        want = jnp.where(lane // rest % 2 == r % 2, MAIN + lane % rest, -1)
+        in_rest = wide[:, 4 * n_main : 4 * n_main + n_rest] == want.astype(F32)
+        for k in range(1, 4):
+            rows = pl.ds((k - 1) * tok, tok)
+            piece = wide[:, k * n_main : (k + 1) * n_main]
             gmat[r, rows, 0:n_main] = jnp.where(in_main, piece, 0.0).astype(BF16)
+            piece = wide[:, 4 * n_main + k * n_rest : 4 * n_main + (k + 1) * n_rest]
             gmat[r, rows, n_main:] = jnp.where(in_rest, piece, 0.0).astype(BF16)
 
     def one_hot(slots, want, e):
@@ -198,30 +212,26 @@
         def _(r):
             route(r)
 
-    sent[META_P].wait_recv()
-    route_range(0, 2)
+    route_range(0, 1)
+    sent[META[1]].wait_recv()
+    route_range(1, 2)
     sent[TO_PARTNER].wait_recv()
     dispatch_pair(0)
-    sent[META_X].wait_recv()
-    sent[META_D].start()
-    sent[META_PX].start()
-    sent[META_Y].wait_recv()
-    sent[META_PY].start()
+    for r in range(2, SOURCES, 2):
+        sent[META[r]].wait_recv()
+        sent[META[r + 1]].start()
+    for r in range(3, SOURCES, 2):
+        sent[META[r]].wait_recv()
+    route_range(2, 5)
     sent[X_LOW].wait_recv()
     sent[DIAG_Y].start()
     sent[Y_HIGH].wait_recv()
     sent[DIAG_X].start()
-    sent[META_D].wait_recv()
-    sent[META_PD].start()
-    sent[META_PX].wait_recv()
-    sent[META_PY].wait_recv()
-    route_range(2, 6)
+    route_range(5, 8)
     sent[X_HIGH].wait_recv()
     sent[PASS_X].start()
     sent[Y_LOW].wait_recv()
     sent[PASS_Y].start()
-    sent[META_PD].wait_recv()
-    route_range(6, 8)
     sent[PASS_X].wait_recv()
     dispatch_pair(1)
     sent[PASS_Y].wait_recv()
@@ -239,30 +249,27 @@
     def up_block(b):
         base = (b * BLOCK) % RING
         for i in range(BLOCK):
-            for copy in load_up(b * BLOCK + i, base + i):
-                copy.wait()
+            wait_up(base + i)
         for i in range(BLOCK):
             e, slot = b * BLOCK + i, base + i
             x = xe[e]
             a = jnp.dot(x, ring[slot, 0, :, 0:full], preferred_element_type=F32)
             u = jnp.dot(x, ring[slot, 1, :, 0:full], preferred_element_type=F32)
-            hid[e, :, 0:full] = (jax.nn.silu(a) * u).astype(BF16)
+            xe[e, :, 0:full] = (jax.nn.silu(a) * u).astype(BF16)
             tail = jnp.concatenate([ring[slot, 0, :, full:], ring[slot, 1, :, full:]], axis=1)
             t = jnp.dot(x, tail, preferred_element_type=F32)
-            hid[e, :, full:] = (jax.nn.silu(t[:, : ff - full]) * t[:, ff - full :]).astype(BF16)
+            xe[e, :, full:ff] = (jax.nn.silu(t[:, : ff - full]) * t[:, ff - full :]).astype(BF16)
 
     ahead = RING // BLOCK
 
-    @pl.loop(0, n_up - ahead)
-    def _(b):
+    for b in range(n_up):
         up_block(b)
-        for i in range(BLOCK):
-            for copy in load_up((b + ahead) * BLOCK + i, (b * BLOCK) % RING + i):
-                copy.start()
-
-    for b in range(n_up - ahead, n_up):
-        up_block(b)
-        start_down(b + ahead)
+        if b + ahead < n_up:
+            for i in range(BLOCK):
+                for copy in load_up((b + ahead) * BLOCK + i, (b * BLOCK) % RING + i):
+                    copy.start()
+        else:
+            start_down(b + ahead)
 
     n_blocks = n_up + per_chunk * (n_chunks - 1) + 1
 
@@ -270,28 +277,25 @@
         c, first = down_block(b)
         column, width = chunks[c]
         step = per_slot if width == WIDE else 2 * per_slot
-        put = (c % 2) * WIDE
         for i in range(lo, hi):
-            for copy in load_down(first + i * step, column, width, (b * BLOCK + i) % RING):
-                copy.wait()
+            wait_down((b * BLOCK + i) % RING)
         for i in range(lo, hi):
             for k in range(step):
                 e = first + i * step + k
                 w = down_view((b * BLOCK + i) % RING, k, width)[...]
-                y = jnp.dot(hid[e], w, preferred_element_type=F32)
-                xe[e, :, put : put + width] = y.astype(BF16)
+                y = jnp.dot(xe[e, :, 0:ff], w, preferred_element_type=F32)
+                xe[e, 0 : MAIN * SOURCES, ff : ff + width] = y[0 : MAIN * SOURCES].astype(BF16)
+                yrest[e, :, 0:width] = y[MAIN * SOURCES :]
         if hi == BLOCK and b + ahead < n_blocks:
             start_down(b + ahead)
 
     def gated(r, c):
         width = chunks[c][1]
-        put = (c % 2) * WIDE
-        top = MAIN * r
-        bottom = MAIN * SOURCES + 4 * rest * (r // 4)
+        top, bottom = MAIN * r, 2 * rest * (r // 2)
         y = jnp.concatenate(
             [
-                xe[:, top : top + MAIN, put : put + width].reshape(n_main, width),
-                xe[:, bottom : bottom + 4 * rest, put : put + width].reshape(n_main, width),
+                xe[:, top : top + MAIN, ff : ff + width].reshape(n_main, width),
+                yrest[:, bottom : bottom + 2 * rest, 0:width].reshape(n_rest, width).astype(BF16),
             ],
             axis=0,
         )
@@ -301,10 +305,15 @@
     def cols(c):
         return pl.ds(*chunks[c])
 
+    last = n_chunks - 1
+
     def sums(kind, c):
         i = FIRST_SUM + 5 * c + kind
         if kind == 0:
             return message(i, away.at[:, :, cols(c)], got.at[:, :, cols(c)], partner)
+        if c == last:
+            place, dev = ((XN, xn), (YN, yn), (DIAG, diag))[kind - 1]
+            return message(i, home.at[place, :, cols(c)], direct.at[kind - 1], dev)
         if kind == 1:
             return message(i, home.at[pl.ds(XN, 2), low, cols(c)], rx1.at[:, :, cols(c)], xn)
         if kind == 2:
@@ -326,8 +335,8 @@
         sums(0, c).wait_recv()
         for d in range(4):
             home[d, :, cols(c)] += got[d, :, cols(c)]
-        sums(1, c).start()
-        sums(2, c).start()
+        for kind in (3, 1, 2) if c == last else (1, 2):
+            sums(kind, c).start()
 
     def pass_on(c):
         sums(1, c).wait_recv()
@@ -337,16 +346,27 @@
         via_x[:, cols(c)] = home[XN, high, cols(c)] + ry1[0, :, cols(c)]
         sums(4, c).start()
 
+    def write(c):
+        return pltpu.make_async_copy(result.at[:, cols(c)], out_hbm.at[:, cols(c)], out_sem.at[c])
+
     def finish(c):
-        sums(3, c).wait_recv()
-        out_ref[low, cols(c)] = (home[OWN, low, cols(c)] + rx1[0, :, cols(c)] + ry2[:, cols(c)]).astype(BF16)
-        sums(4, c).wait_recv()
-        out_ref[high, cols(c)] = (home[OWN, high, cols(c)] + ry1[1, :, cols(c)] + rx2[:, cols(c)]).astype(BF16)
+        if c == last:
+            total = home[OWN, :, cols(c)]
+            for kind in (1, 2, 3):
+                sums(kind, c).wait_recv()
+                total += direct[kind - 1]
+            result[:, cols(c)] = total.astype(BF16)
+        else:
+            sums(3, c).wait_recv()
+            result[low, cols(c)] = (home[OWN, low, cols(c)] + rx1[0, :, cols(c)] + ry2[:, cols(c)]).astype(BF16)
+            sums(4, c).wait_recv()
+            result[high, cols(c)] = (home[OWN, high, cols(c)] + ry1[1, :, cols(c)] + rx2[:, cols(c)]).astype(BF16)
+        write(c).start()
 
     b = n_up
     for c in range(n_chunks):
         if c < n_chunks - 1:
-            parts = [(b + i, 0, BLOCK) for i in range(per_chunk)]
+            parts = [(b, 0, BLOCK // 2), (b, BLOCK // 2, BLOCK)] + [(b + i, 0, BLOCK) for i in range(1, per_chunk)]
             b += per_chunk
         else:
             parts = [(b, 0, BLOCK // 2), (b, BLOCK // 2, BLOCK)]
@@ -358,20 +378,20 @@
                 pass_on(c - 2)
         combine_away(c)
         combine_home(c)
-    last = n_chunks - 1
+    finish(0)
     chip_sum(last)
     pass_on(last - 1)
-    for c in range(last - 1):
+    for c in range(1, last - 1):
         finish(c)
-    pass_on(last)
+    finish(last)
     finish(last - 1)
-    finish(last)
-
-    for i in range(FIRST_SUM):
+
+    for i in range(1, FIRST_SUM):
         sent[i].wait_send()
     for c in range(n_chunks):
-        for kind in range(5):
+        for kind in range(4 if c == last else 5):
             sums(kind, c).wait_send()
+        write(c).wait()
 
 
 def solution(mesh):
@@ -384,25 +404,26 @@
         experts, _, ff = w_gate.shape
         capacity = 5 * top_k * tok // (4 * experts * ep_size)
         assert (ep_size, tp_size, capacity, tok, experts) == (2, 4, MAIN + 4, 128, 32)
-        n_main = experts * MAIN
+        n_main, n_rest = experts * MAIN, experts * 8
         rows = SOURCES * capacity
         n_chunks = -(-d_model // WIDE)
         n_msg = FIRST_SUM + 5 * n_chunks
-        vmem = pl.BlockSpec(memory_space=pltpu.VMEM)
         hbm = pl.BlockSpec(memory_space=pl.ANY)
         return pl.pallas_call(
             kernel,
             out_shape=jax.ShapeDtypeStruct((tok, d_model), BF16),
-            in_specs=[vmem, vmem, hbm, hbm, hbm, hbm],
-            out_specs=vmem,
+            in_specs=[hbm] * 6,
+            out_specs=hbm,
             scratch_shapes=[
+                pltpu.VMEM((top_k, tok), jnp.int32),
+                pltpu.VMEM((top_k, tok), F32),
                 pltpu.VMEM((SOURCES, tok, d_model), BF16),
                 pltpu.VMEM((SOURCES, 2 * top_k, tok), F32),
                 pltpu.VMEM((SOURCES, experts, tok), F32),
-                pltpu.VMEM((4 * experts, 4 * n_main), BF16),
-                pltpu.VMEM((SOURCES, 3 * tok, 2 * n_main), BF16),
+                pltpu.VMEM((4 * experts, 4 * (n_main + n_rest)), BF16),
+                pltpu.VMEM((SOURCES, 3 * tok, n_main + n_rest), BF16),
                 pltpu.VMEM((experts, rows, d_model), BF16),
-                pltpu.VMEM((experts, rows, ff), BF16),
+                pltpu.VMEM((experts, rows - MAIN * SOURCES, WIDE), F32),
                 pltpu.VMEM((RING, 2, d_model, ff), BF16),
                 pltpu.VMEM((4, tok, d_model), F32),
                 pltpu.VMEM((4, tok, d_model), F32),
@@ -413,8 +434,11 @@
                 pltpu.VMEM((tok // 2, d_model), F32),
                 pltpu.VMEM((tok // 2, d_model), F32),
                 pltpu.VMEM((tok // 2, d_model), F32),
-                pltpu.SemaphoreType.DMA,
-                pltpu.SemaphoreType.DMA((RING, 8)),
+                pltpu.VMEM((3, tok, d_model - WIDE * (n_chunks - 1)), F32),
+                pltpu.VMEM((tok, d_model), BF16),
+                pltpu.SemaphoreType.DMA((3,)),
+                pltpu.SemaphoreType.DMA((n_chunks,)),
+                pltpu.SemaphoreType.DMA((RING,)),
                 pltpu.SemaphoreType.DMA((n_msg,)),
                 pltpu.SemaphoreType.DMA((n_msg,)),
             ],

time: 73.8 us -> 59.6 us (0.81)
  Pallas kernels: 71.9 us -> 57.8 us
    pallas_call x1, Pallas kernels: 71.9 us -> 57.8 us  [local_layer(): pl.pallas_call(kernel, out_shape=jax.ShapeDtypeStruct((tok, d_model), BF1...]
where the time goes in v2:
time: 59.6 us; the launch traced here: 59.5 us
  Pallas kernels  57.8 us (97%)
  local copies, waits for them, and re-layouts  1.65 us (3%)
    pallas_call x1, Pallas kernels, local_layer(): pl.pallas_call(kernel, out_shape=jax.ShapeDtypeStruct((tok, d_model), BF1...  57.8 us
    unnamed x1, local copies, waits for them, and re-layouts  1.65 us

profile of v2, /device:TPU:0, one launch (start us, length us, event | category | flops | bytes accessed | tf_op | source)
XLA Modules:
  0.0 59.5 jit_solution(6847207677051810273)
XLA Ops:
  0.0 57.8 %shard_map.64 = bf16[128,896]{1,0:T(8,128)(2,1)} custom-call(s32[8,128]{1,0:T(8,128)} %bitcast.2, f32[8,128]{1,0:T(8,128)} %bitcast.3, bf16[128,896]{1,0:T(8,128)(2,1)} %tok_hbm.1, bf16[32,896,640]{2,1,0:T(8,128)(2,1)} %wg_hbm.1, bf16[32,896,640]{2,1,0:T(8,128)(2,1)} %wu_hbm.1, bf16[32,640,896]{2,1,0:T(8,128)(2,1)} %wd_hbm.1), custom_call_target="tpu_custom_call" | custom-call | tf_op jit(solution)/shard_map/pallas_call | solution.py:412
  57.8 1.6 %copy.8 = bf16[128,896]{1,0:T(8,128)(2,1)} copy(bf16[128,896]{1,0:T(8,128)(2,1)} %shard_map.64) | data formatting | bytes 458752

commit v3 on v2

--- a/solution.py
+++ b/solution.py
@@ -186,26 +186,33 @@
         line = jnp.broadcast_to(slots[e : e + 1, :], want.shape)
         return jnp.where(line == want, 1.0, 0.0).astype(BF16)
 
-    def dispatch(sources, want, rows, batch):
-        slots = jnp.concatenate([val[r] for r in sources], axis=1)
+    def dispatch(sources, want, rows, batch, held=None):
+        slots = jnp.concatenate([val[r] for r in sources], axis=1) if len(sources) > 1 else val[sources[0]]
         x = xg[sources[0] : sources[-1] + 1].reshape(len(sources) * tok, d_model)
         height = want.shape[0]
         for e in range(0, experts, batch):
             pick = jnp.concatenate([one_hot(slots, want, e + i) for i in range(batch)], axis=0)
-            placed = jnp.dot(pick, x, preferred_element_type=F32).astype(BF16)
-            xe[e : e + batch, rows : rows + height, :] = placed.reshape(batch, height, d_model)
-
-    def dispatch_pair(p):
-        shape = (2 * MAIN, 2 * tok)
+            placed = jnp.dot(pick, x, preferred_element_type=F32)
+            part = slice(e * height // tok, (e + batch) * height // tok)
+            if held == "keep":
+                away[part] = placed.reshape(-1, tok, d_model)
+                continue
+            if held == "add":
+                placed += away[part].reshape(placed.shape)
+            xe[e : e + batch, rows : rows + height, :] = placed.astype(BF16).reshape(batch, height, d_model)
+
+    def dispatch_main(*sources):
+        shape = (len(sources) * MAIN, len(sources) * tok)
         i, l = iota(shape, 0), iota(shape, 1)
         want = jnp.where(i // MAIN == l // tok, i % MAIN, -1).astype(F32)
-        dispatch([2 * p, 2 * p + 1], want, 2 * MAIN * p, 8)
-
-    def dispatch_rest(q):
-        shape = (4 * rest, 4 * tok)
+        dispatch(sources, want, MAIN * sources[0], 16 // len(sources))
+
+    def dispatch_rest(sources, held=None):
+        q = sources[0] // 4
+        shape = (4 * rest, len(sources) * tok)
         i, l = iota(shape, 0), iota(shape, 1)
-        want = jnp.where(i // rest == l // tok, MAIN + i % rest, -1).astype(F32)
-        dispatch([4 * q + i for i in range(4)], want, MAIN * SOURCES + 4 * rest * q, 16)
+        want = jnp.where(4 * q + i // rest == sources[0] + l // tok, MAIN + i % rest, -1).astype(F32)
+        dispatch(sources, want, MAIN * SOURCES + 4 * rest * q, 16, held)
 
     def route_range(lo, hi):
         @pl.loop(lo, hi)
@@ -216,7 +223,7 @@
     sent[META[1]].wait_recv()
     route_range(1, 2)
     sent[TO_PARTNER].wait_recv()
-    dispatch_pair(0)
+    dispatch_main(0, 1)
     for r in range(2, SOURCES, 2):
         sent[META[r]].wait_recv()
         sent[META[r + 1]].start()
@@ -232,17 +239,21 @@
     sent[PASS_X].start()
     sent[Y_LOW].wait_recv()
     sent[PASS_Y].start()
+    dispatch_main(2)
+    dispatch_main(4)
     sent[PASS_X].wait_recv()
-    dispatch_pair(1)
+    dispatch_main(3)
     sent[PASS_Y].wait_recv()
-    dispatch_pair(2)
+    dispatch_main(5)
+    dispatch_rest((0, 1, 2, 3))
     sent[DIAG_Y].wait_recv()
     sent[DIAG_X].wait_recv()
     sent[PASS_D].start()
-    dispatch_rest(0)
+    dispatch_rest((4, 5), "keep")
+    dispatch_main(6)
     sent[PASS_D].wait_recv()
-    dispatch_pair(3)
-    dispatch_rest(1)
+    dispatch_main(7)
+    dispatch_rest((6, 7), "add")
 
     full = ff // WIDE * WIDE
 
@@ -271,14 +282,16 @@
         else:
             start_down(b + ahead)
 
+    def wait_block(b, lo=0, hi=BLOCK):
+        for i in range(lo, hi):
+            wait_down((b * BLOCK + i) % RING)
+
     n_blocks = n_up + per_chunk * (n_chunks - 1) + 1
 
     def down(b, lo, hi):
         c, first = down_block(b)
         column, width = chunks[c]
         step = per_slot if width == WIDE else 2 * per_slot
-        for i in range(lo, hi):
-            wait_down((b * BLOCK + i) % RING)
         for i in range(lo, hi):
             for k in range(step):
                 e = first + i * step + k
@@ -363,19 +376,29 @@
             result[high, cols(c)] = (home[OWN, high, cols(c)] + ry1[1, :, cols(c)] + rx2[:, cols(c)]).astype(BF16)
         write(c).start()
 
-    b = n_up
+    def blocks(c):
+        return range(n_up + c * per_chunk, min(n_up + (c + 1) * per_chunk, n_blocks))
+
     for c in range(n_chunks):
-        if c < n_chunks - 1:
-            parts = [(b, 0, BLOCK // 2), (b, BLOCK // 2, BLOCK)] + [(b + i, 0, BLOCK) for i in range(1, per_chunk)]
-            b += per_chunk
+        first, *others = blocks(c)
+        if c == 0:
+            wait_block(first)
+            down(first, 0, BLOCK)
         else:
-            parts = [(b, 0, BLOCK // 2), (b, BLOCK // 2, BLOCK)]
-        for n, part in enumerate(parts):
-            down(*part)
-            if n == 0 and c >= 1:
-                chip_sum(c - 1)
-            if n == 1 and c >= 2:
-                pass_on(c - 2)
+            cut = BLOCK // 2 if c < last else BLOCK // 4
+            wait_block(first, 0, cut)
+            down(first, 0, cut)
+            chip_sum(c - 1)
+            wait_block(first, cut, BLOCK)
+            for b in others:
+                wait_block(b)
+            down(first, cut, BLOCK)
+        for b in others:
+            if c == 0:
+                wait_block(b)
+            down(b, 0, BLOCK)
+        if c >= 2:
+            pass_on(c - 2)
         combine_away(c)
         combine_home(c)
     finish(0)

time: 59.6 us -> 58.3 us (0.978)
  Pallas kernels: 57.8 us -> 56.5 us
    pallas_call x1, Pallas kernels: 57.8 us -> 56.5 us  [local_layer(): pl.pallas_call(kernel, out_shape=jax.ShapeDtypeStruct((tok, d_model), BF1...]
where the time goes in v3:
time: 58.3 us; the launch traced here: 58.1 us
  Pallas kernels  56.5 us (97%)
  local copies, waits for them, and re-layouts  1.65 us (3%)
    pallas_call x1, Pallas kernels, local_layer(): pl.pallas_call(kernel, out_shape=jax.ShapeDtypeStruct((tok, d_model), BF1...  56.5 us
    unnamed x1, local copies, waits for them, and re-layouts  1.65 us

profile of v3, /device:TPU:0, one launch (start us, length us, event | category | flops | bytes accessed | tf_op | source)
XLA Modules:
  0.0 58.1 jit_solution(3744312388756658067)
XLA Ops:
  0.0 56.5 %shard_map.64 = bf16[128,896]{1,0:T(8,128)(2,1)} custom-call(s32[8,128]{1,0:T(8,128)} %bitcast.2, f32[8,128]{1,0:T(8,128)} %bitcast.3, bf16[128,896]{1,0:T(8,128)(2,1)} %tok_hbm.1, bf16[32,896,640]{2,1,0:T(8,128)(2,1)} %wg_hbm.1, bf16[32,896,640]{2,1,0:T(8,128)(2,1)} %wu_hbm.1, bf16[32,640,896]{2,1,0:T(8,128)(2,1)} %wd_hbm.1), custom_call_target="tpu_custom_call" | custom-call | tf_op jit(solution)/shard_map/pallas_call | solution.py:435
  56.5 1.6 %copy.8 = bf16[128,896]{1,0:T(8,128)(2,1)} copy(bf16[128,896]{1,0:T(8,128)(2,1)} %shard_map.64) | data formatting | bytes 458752

commit v4 on v3

--- a/solution.py
+++ b/solution.py
@@ -21,6 +21,7 @@
 META = range(8)
 TO_PARTNER, X_LOW, X_HIGH, Y_HIGH, Y_LOW, DIAG_Y, DIAG_X, PASS_X, PASS_Y, PASS_D = range(8, 18)
 FIRST_SUM = 18
+META_SENT, ROWS_SENT, SUM_SENT, LAST_SENT = 0, 1, 2, 7
 OWN, XN, DIAG, YN = range(4)
 PLACE = (OWN, XN, YN, DIAG)
 
@@ -109,28 +110,28 @@
     for copy in mine:
         copy.start()
 
-    def message(i, src, dst, dev):
+    def message(i, src, dst, dev, group):
         return pltpu.make_async_remote_copy(
-            src_ref=src, dst_ref=dst, send_sem=ssem.at[i], recv_sem=rsem.at[i], device_id=dev, device_id_type=MESH
+            src_ref=src, dst_ref=dst, send_sem=ssem.at[group], recv_sem=rsem.at[i], device_id=dev, device_id_type=MESH
         )
 
     low, high = pl.ds(0, half), pl.ds(half, half)
     sent = {
-        TO_PARTNER: message(TO_PARTNER, xg.at[0], xg.at[1], partner),
-        X_LOW: message(X_LOW, xg.at[0, low], xg.at[2, low], xn),
-        X_HIGH: message(X_HIGH, xg.at[0, high], xg.at[2, high], xn),
-        Y_HIGH: message(Y_HIGH, xg.at[0, high], xg.at[4, high], yn),
-        Y_LOW: message(Y_LOW, xg.at[0, low], xg.at[4, low], yn),
-        DIAG_Y: message(DIAG_Y, xg.at[2, low], xg.at[6, low], yn),
-        DIAG_X: message(DIAG_X, xg.at[4, high], xg.at[6, high], xn),
-        PASS_X: message(PASS_X, xg.at[2], xg.at[3], partner),
-        PASS_Y: message(PASS_Y, xg.at[4], xg.at[5], partner),
-        PASS_D: message(PASS_D, xg.at[6], xg.at[7], partner),
+        TO_PARTNER: message(TO_PARTNER, xg.at[0], xg.at[1], partner, ROWS_SENT),
+        X_LOW: message(X_LOW, xg.at[0, low], xg.at[2, low], xn, ROWS_SENT),
+        X_HIGH: message(X_HIGH, xg.at[0, high], xg.at[2, high], xn, ROWS_SENT),
+        Y_HIGH: message(Y_HIGH, xg.at[0, high], xg.at[4, high], yn, ROWS_SENT),
+        Y_LOW: message(Y_LOW, xg.at[0, low], xg.at[4, low], yn, ROWS_SENT),
+        DIAG_Y: message(DIAG_Y, xg.at[2, low], xg.at[6, low], yn, ROWS_SENT),
+        DIAG_X: message(DIAG_X, xg.at[4, high], xg.at[6, high], xn, ROWS_SENT),
+        PASS_X: message(PASS_X, xg.at[2], xg.at[3], partner, ROWS_SENT),
+        PASS_Y: message(PASS_Y, xg.at[4], xg.at[5], partner, ROWS_SENT),
+        PASS_D: message(PASS_D, xg.at[6], xg.at[7], partner, ROWS_SENT),
     }
 
     for r in range(1, SOURCES):
         hop = r == 1 or r % 2 == 0
-        sent[META[r]] = message(META[r], mg.at[0 if hop else r - 1], mg.at[r], device[r] if hop else partner)
+        sent[META[r]] = message(META[r], mg.at[0 if hop else r - 1], mg.at[r], device[r] if hop else partner, META_SENT)
 
     for copy in mine:
         copy.wait()
@@ -322,18 +323,19 @@
 
     def sums(kind, c):
         i = FIRST_SUM + 5 * c + kind
+        group = SUM_SENT + kind
         if kind == 0:
-            return message(i, away.at[:, :, cols(c)], got.at[:, :, cols(c)], partner)
+            return message(i, away.at[:, :, cols(c)], got.at[:, :, cols(c)], partner, group)
         if c == last:
             place, dev = ((XN, xn), (YN, yn), (DIAG, diag))[kind - 1]
-            return message(i, home.at[place, :, cols(c)], direct.at[kind - 1], dev)
+            return message(i, home.at[place, :, cols(c)], direct.at[kind - 1], dev, LAST_SENT)
         if kind == 1:
-            return message(i, home.at[pl.ds(XN, 2), low, cols(c)], rx1.at[:, :, cols(c)], xn)
+            return message(i, home.at[pl.ds(XN, 2), low, cols(c)], rx1.at[:, :, cols(c)], xn, group)
         if kind == 2:
-            return message(i, home.at[pl.ds(DIAG, 2), high, cols(c)], ry1.at[:, :, cols(c)], yn)
+            return message(i, home.at[pl.ds(DIAG, 2), high, cols(c)], ry1.at[:, :, cols(c)], yn, group)
         if kind == 3:
-            return message(i, via_y.at[:, cols(c)], ry2.at[:, cols(c)], yn)
-        return message(i, via_x.at[:, cols(c)], rx2.at[:, cols(c)], xn)
+            return message(i, via_y.at[:, cols(c)], ry2.at[:, cols(c)], yn, group)
+        return message(i, via_x.at[:, cols(c)], rx2.at[:, cols(c)], xn, group)
 
     def combine_away(c):
         for r in range(1, SOURCES, 2):
@@ -360,7 +362,7 @@
         sums(4, c).start()
 
     def write(c):
-        return pltpu.make_async_copy(result.at[:, cols(c)], out_hbm.at[:, cols(c)], out_sem.at[c])
+        return pltpu.make_async_copy(result.at[:, cols(c)], out_hbm.at[:, cols(c)], out_sem)
 
     def finish(c):
         if c == last:
@@ -409,12 +411,19 @@
     finish(last)
     finish(last - 1)
 
-    for i in range(1, FIRST_SUM):
-        sent[i].wait_send()
-    for c in range(n_chunks):
-        for kind in range(4 if c == last else 5):
-            sums(kind, c).wait_send()
-        write(c).wait()
+    most = pl.ds(0, chunks[last][0])
+    for group, ref in (
+        (META_SENT, mg.at[pl.ds(0, SOURCES - 1)]),
+        (ROWS_SENT, xg.at[pl.ds(0, SOURCES - 1)]),
+        (SUM_SENT, away),
+        (SUM_SENT + 1, home.at[pl.ds(XN, 2), low, most]),
+        (SUM_SENT + 2, home.at[pl.ds(DIAG, 2), high, most]),
+        (SUM_SENT + 3, via_y.at[:, most]),
+        (SUM_SENT + 4, via_x.at[:, most]),
+        (LAST_SENT, home.at[pl.ds(XN, 3), :, cols(last)]),
+    ):
+        message(0, ref, ref, partner, group).wait_send()
+    pltpu.make_async_copy(result, out_hbm, out_sem).wait()
 
 
 def solution(mesh):
@@ -460,9 +469,9 @@
                 pltpu.VMEM((3, tok, d_model - WIDE * (n_chunks - 1)), F32),
                 pltpu.VMEM((tok, d_model), BF16),
                 pltpu.SemaphoreType.DMA((3,)),
-                pltpu.SemaphoreType.DMA((n_chunks,)),
+                pltpu.SemaphoreType.DMA,
                 pltpu.SemaphoreType.DMA((RING,)),
-                pltpu.SemaphoreType.DMA((n_msg,)),
+                pltpu.SemaphoreType.DMA((LAST_SENT + 1,)),
                 pltpu.SemaphoreType.DMA((n_msg,)),
             ],
             compiler_params=pltpu.CompilerParams(

time: 58.3 us -> 57.9 us (level)
  no operation moved by 1% of the time
where the time goes in v4:
time: 57.9 us; the launch traced here: 57.8 us
  Pallas kernels  56.1 us (97%)
  local copies, waits for them, and re-layouts  1.65 us (3%)
    pallas_call x1, Pallas kernels, local_layer(): pl.pallas_call(kernel, out_shape=jax.ShapeDtypeStruct((tok, d_model), BF1...  56.1 us
    unnamed x1, local copies, waits for them, and re-layouts  1.65 us

profile of v4, /device:TPU:0, one launch (start us, length us, event | category | flops | bytes accessed | tf_op | source)
XLA Modules:
  0.0 57.8 jit_solution(6492260406759438295)
XLA Ops:
  0.0 56.1 %shard_map.64 = bf16[128,896]{1,0:T(8,128)(2,1)} custom-call(s32[8,128]{1,0:T(8,128)} %bitcast.2, f32[8,128]{1,0:T(8,128)} %bitcast.3, bf16[128,896]{1,0:T(8,128)(2,1)} %tok_hbm.1, bf16[32,896,640]{2,1,0:T(8,128)(2,1)} %wg_hbm.1, bf16[32,896,640]{2,1,0:T(8,128)(2,1)} %wu_hbm.1, bf16[32,640,896]{2,1,0:T(8,128)(2,1)} %wd_hbm.1), custom_call_target="tpu_custom_call" | custom-call | tf_op jit(solution)/shard_map/pallas_call | solution.py:444
  56.1 1.6 %copy.8 = bf16[128,896]{1,0:T(8,128)(2,1)} copy(bf16[128,896]{1,0:T(8,128)(2,1)} %shard_map.64) | data formatting | bytes 458752
